TPU v7x, 32 devices: a whole 2x2x4 slice. The times are simulated.
32 devices in a mesh: dp: 4 (over y, x), centers: 8 (over z, core).
Axes of the slice: x: 2, y: 2, z: 4, core: 2. Of those that a mesh axis runs over, the one named last changes fastest.
Arguments:
- points: bfloat16 [16384, 32], P('dp'), may hold values from -6 to 6
- centers: bfloat16 [16384, 32], P('centers'), may hold values from -6 to 6
- coef: bfloat16 [16384, 64], P('centers'), may hold values from -0.1875 to 0.1875
Outputs:
- product: float32 [16384, 64], P('centers')
All inputs are finite; a program needn't handle non-finite values.
Results may differ from a plain program's by a relative error of at most 0.0003.
Values may be sent and summed in bfloat16 or wider, within the bound.
No kernel may reach another device: no remote copies, remote signals or barrier semaphores. Data moves between devices by JAX's collectives and lax.ppermute only.
A program may use at most 128 MiB of HBM per device.

v0:
```python
import jax
import jax.numpy as jnp
from jax import lax
from jax.sharding import PartitionSpec as P


def kernel_block(left_pts, left_sq, right_pts, right_sq, features):
    inner = lax.dot_general(
        left_pts, right_pts, (((1,), (1,)), ((), ())), preferred_element_type=jnp.float32
    )
    dist = left_sq[:, None] + right_sq[None, :] - 2.0 * inner
    return jnp.exp(dist * (-2.0 / features)).astype(jnp.bfloat16)


def squares(values):
    wide = values.astype(jnp.float32)
    return jnp.sum(wide * wide, axis=1)


def on_device(points, centers, coef):
    features = points.shape[1]
    local_pts = points.shape[0]
    local_cen = centers.shape[0]
    outs_count = coef.shape[1]
    block_pts = min(1024, local_pts)
    block_count = local_pts // block_pts
    cen_sq = squares(centers)
    point_blocks = points.reshape(block_count, block_pts, features)
    scalar_zero = jnp.zeros((), jnp.float32)

    def forward_keep(carry, block):
        kernel = kernel_block(block, squares(block), centers, cen_sq, features)
        return (carry, (kernel, jnp.dot(kernel, coef, preferred_element_type=jnp.float32)))

    unused, (tiles, partial_value) = lax.scan(forward_keep, scalar_zero, point_blocks)
    forward_part = partial_value.reshape(local_pts, outs_count)
    shared = lax.psum_scatter(
        forward_part.astype(jnp.bfloat16), "centers", scatter_dimension=0, tiled=True
    )
    forward = lax.all_gather(shared, "centers", axis=0, tiled=True)
    forward_blocks = forward.reshape(block_count, block_pts, outs_count)
    back = jnp.einsum("bij,bio->jo", tiles, forward_blocks, preferred_element_type=jnp.float32)
    total_pts = local_pts * lax.axis_size("dp")
    back = back * (1.0 / jnp.sqrt(jnp.float32(total_pts)))
    own_count = local_cen // lax.axis_size("dp")
    own_start = lax.axis_index("dp") * own_count
    own_cen = lax.dynamic_slice_in_dim(centers, own_start, own_count, 0)
    own_sq = squares(own_cen)
    piece_cen = lax.all_gather(centers, "centers", axis=0, tiled=True)
    piece_coef = lax.all_gather(coef, "centers", axis=0, tiled=True)
    kernel = kernel_block(own_cen, own_sq, piece_cen, squares(piece_cen), features)
    regular = jnp.dot(kernel, piece_coef, preferred_element_type=jnp.float32)
    placed = lax.dynamic_update_slice_in_dim(jnp.zeros_like(back), regular, own_start, 0)
    return lax.psum(back + placed, "dp")


def solution(mesh):
    in_specs = (P("dp", None), P("centers", None), P("centers", None))
    out_specs = P("centers", None)
    return jax.shard_map(
        on_device, mesh=mesh, in_specs=in_specs, out_specs=out_specs, check_vma=False
    )
```

profile of v0, /device:TPU:0, one launch (start us, length us, event | category | flops | bytes accessed | tf_op | source)
XLA Modules:
  0.0 192.9 jit_solution(11572367523075643524)
XLA Ops:
  6.5 1.4 copy.5
  8.0 1.0 multiply_reduce_fusion.2
  8.9 27.9 %while.12 = (s32[]{:T(128)}, bf16[4,1024,2048]{2,1,0:T(8,128)(2,1)}, bf16[4,1024,64]{1,2,0:T(8,128)(2,1)S(1)}, bf16[4,1024,32]{2,1,0:T(8,128)(2,1)S(1)}, f32[204...) while((s32[]{:T(128)}, bf16[4,1024,2048]{2,1,0:T(8,128)(2,1)}, ...), condition=%wide.region_3.4_spmd, body=%wide.region_1.3_spmd.sunk | while | flops 413236224 | bytes 13583461 | solution.py:35
  9.2 4.4 %bitcast_dynamic-update-slice_fusion.2 = (bf16[4,1024,2048]{2,1,0:T(8,128)(2,1)}, bf16[1024,2048]{1,0:T(8,128)(2,1)S(1)}) fusion(bf16[4,1024,2048]{2,1,0:T(8,128)(2,1)} %get-tuple-element.117, s32[]{:T(128)S(6)} %copy.19, bf16[2048,32]{0,1:T(8,128)(2,1)} %get-tuple-element.129, bf16[4,1024,32]{2,1,0:T(8,128)(2,1)S(1)} %get-tuple-element.127, ...), kind=kOutput, calls=%fused_computation.1.clone.1 | convolution fusion | flops 144703488 | bytes 8795136 | tf_op jit(solution)/shard_map/while/body/eval_jaxpr/dot_general | solution.py:8
  13.5 2.3 %fusion.29 = bf16[4,1024,64]{1,2,0:T(8,128)(2,1)S(1)} fusion(bf16[4,1024,64]{1,2,0:T(8,128)(2,1)S(1)} %get-tuple-element.118, s32[]{:T(128)S(6)} %copy.19, bf16[1024,2048]{1,0:T(8,128)(2,1)S(1)} %get-tuple-element.107, bf16[2048,64]{0,1:T(8,128)(2,1)} %get-tuple-element.130), kind=kOutput, calls=%fused_computation.3.clone.1 | convolution fusion | flops 268435456 | bytes 4718596 | tf_op jit(solution)/shard_map/while/body/eval_jaxpr/dot_general | solution.py:33
  16.1 4.4 %bitcast_dynamic-update-slice_fusion.2 = (bf16[4,1024,2048]{2,1,0:T(8,128)(2,1)}, bf16[1024,2048]{1,0:T(8,128)(2,1)S(1)}) fusion(bf16[4,1024,2048]{2,1,0:T(8,128)(2,1)} %get-tuple-element.117, s32[]{:T(128)S(6)} %copy.19, bf16[2048,32]{0,1:T(8,128)(2,1)} %get-tuple-element.129, bf16[4,1024,32]{2,1,0:T(8,128)(2,1)S(1)} %get-tuple-element.127, ...), kind=kOutput, calls=%fused_computation.1.clone.1 | convolution fusion | flops 144703488 | bytes 8795136 | tf_op jit(solution)/shard_map/while/body/eval_jaxpr/dot_general | solution.py:8
  20.5 2.3 %fusion.29 = bf16[4,1024,64]{1,2,0:T(8,128)(2,1)S(1)} fusion(bf16[4,1024,64]{1,2,0:T(8,128)(2,1)S(1)} %get-tuple-element.118, s32[]{:T(128)S(6)} %copy.19, bf16[1024,2048]{1,0:T(8,128)(2,1)S(1)} %get-tuple-element.107, bf16[2048,64]{0,1:T(8,128)(2,1)} %get-tuple-element.130), kind=kOutput, calls=%fused_computation.3.clone.1 | convolution fusion | flops 268435456 | bytes 4718596 | tf_op jit(solution)/shard_map/while/body/eval_jaxpr/dot_general | solution.py:33
  23.1 4.4 %bitcast_dynamic-update-slice_fusion.2 = (bf16[4,1024,2048]{2,1,0:T(8,128)(2,1)}, bf16[1024,2048]{1,0:T(8,128)(2,1)S(1)}) fusion(bf16[4,1024,2048]{2,1,0:T(8,128)(2,1)} %get-tuple-element.117, s32[]{:T(128)S(6)} %copy.19, bf16[2048,32]{0,1:T(8,128)(2,1)} %get-tuple-element.129, bf16[4,1024,32]{2,1,0:T(8,128)(2,1)S(1)} %get-tuple-element.127, ...), kind=kOutput, calls=%fused_computation.1.clone.1 | convolution fusion | flops 144703488 | bytes 8795136 | tf_op jit(solution)/shard_map/while/body/eval_jaxpr/dot_general | solution.py:8
  27.5 2.3 %fusion.29 = bf16[4,1024,64]{1,2,0:T(8,128)(2,1)S(1)} fusion(bf16[4,1024,64]{1,2,0:T(8,128)(2,1)S(1)} %get-tuple-element.118, s32[]{:T(128)S(6)} %copy.19, bf16[1024,2048]{1,0:T(8,128)(2,1)S(1)} %get-tuple-element.107, bf16[2048,64]{0,1:T(8,128)(2,1)} %get-tuple-element.130), kind=kOutput, calls=%fused_computation.3.clone.1 | convolution fusion | flops 268435456 | bytes 4718596 | tf_op jit(solution)/shard_map/while/body/eval_jaxpr/dot_general | solution.py:33
  30.1 4.4 %bitcast_dynamic-update-slice_fusion.2 = (bf16[4,1024,2048]{2,1,0:T(8,128)(2,1)}, bf16[1024,2048]{1,0:T(8,128)(2,1)S(1)}) fusion(bf16[4,1024,2048]{2,1,0:T(8,128)(2,1)} %get-tuple-element.117, s32[]{:T(128)S(6)} %copy.19, bf16[2048,32]{0,1:T(8,128)(2,1)} %get-tuple-element.129, bf16[4,1024,32]{2,1,0:T(8,128)(2,1)S(1)} %get-tuple-element.127, ...), kind=kOutput, calls=%fused_computation.1.clone.1 | convolution fusion | flops 144703488 | bytes 8795136 | tf_op jit(solution)/shard_map/while/body/eval_jaxpr/dot_general | solution.py:8
  34.5 2.3 %fusion.29 = bf16[4,1024,64]{1,2,0:T(8,128)(2,1)S(1)} fusion(bf16[4,1024,64]{1,2,0:T(8,128)(2,1)S(1)} %get-tuple-element.118, s32[]{:T(128)S(6)} %copy.19, bf16[1024,2048]{1,0:T(8,128)(2,1)S(1)} %get-tuple-element.107, bf16[2048,64]{0,1:T(8,128)(2,1)} %get-tuple-element.130), kind=kOutput, calls=%fused_computation.3.clone.1 | convolution fusion | flops 268435456 | bytes 4718596 | tf_op jit(solution)/shard_map/while/body/eval_jaxpr/dot_general | solution.py:33
  36.8 0.8 copy.9
  37.7 0.7 all-gather.3.cloned.1.call-update
  38.5 0.7 all-gather.5.cloned.1.call-update
  39.2 0.8 multiply_reduce_fusion.3
  40.0 31.9 %reduce-scatter.2.cloned.1.call-done = bf16[512,64]{0,1:T(8,128)(2,1)} async-done(((bf16[4096,64]{0,1:T(8,128)(2,1)}), bf16[512,64]{0,1:T(8,128)(2,1)}) %reduce-scatter.2.cloned.1.call-update) | async-done | bytes 65552 | tf_op jit(solution)/shard_map/reduce_scatter | solution.py:37
  71.9 16.8 %all_gather.9 = bf16[4096,64]{0,1:T(8,128)(2,1)S(1)} all-gather(bf16[512,64]{0,1:T(8,128)(2,1)} %reduce-scatter.2.cloned.1.call-done), channel_id=1, replica_groups=mesh['dp'=4,'centers'=8] {'centers'}, dimensions={0}, use_global_device_ids=true | all-gather | bytes 589824 | tf_op jit(solution)/shard_map/all_gather | solution.py:40
  88.7 8.9 %fusion.5 = f32[2048,64]{0,1:T(8,128)S(1)} fusion(bf16[4,1024,2048]{2,1,0:T(8,128)(2,1)} %get-tuple-element.43, bf16[8,4,8,1024]{3,2,1,0:T(8,128)(2,1)S(1)} %bitcast.46), kind=kOutput, calls=%fused_computation.11 | convolution fusion | flops 1073872896 | bytes 17825792 | tf_op jit(solution)/shard_map/bij,bio->jo/dot_general | solution.py:42
  97.6 1.5 multiply_reduce_fusion.1
  99.2 26.4 %all-gather.5.cloned.1.call-done = bf16[16384,64]{0,1:T(8,128)(2,1)} async-done(((bf16[2048,64]{0,1:T(8,128)(2,1)}), bf16[16384,64]{0,1:T(8,128)(2,1)}) %all-gather.5.cloned.1.call-update) | async-done | bytes 2097168 | tf_op jit(solution)/shard_map/all_gather | solution.py:50
  125.6 13.2 %fusion.7 = f32[2048,64]{0,1:T(8,128)S(1)} fusion(f32[2048,64]{0,1:T(8,128)S(1)} %fusion.5, s32[]{:T(128)S(6)} %select_n.4, bf16[16384,64]{0,1:T(8,128)(2,1)} %all-gather.5.cloned.1.call-done, bf16[16384,32]{0,1:T(8,128)(2,1)} %all-gather.3.cloned.1.call-done, f32[16384]{0:T(1024)S(1)} %multiply_reduce_fusion.1, f32[512]{0:T(512)S(1)} %multiply_reduce_fusion.3, ...), kind=kOutput, calls=%fused_computation.14 | convolution fusion | flops 1652588544 | bytes 3509248 | tf_op jit(solution)/shard_map/dot_general | solution.py:52
  138.8 0.8 copy-done
  139.6 44.9 %all-reduce.2.cloned.1.call-done = f32[2048,64]{0,1:T(8,128)} async-done(((f32[2048,64]{0,1:T(8,128)}), f32[2048,64]{0,1:T(8,128)}) %all-reduce.2.cloned.1.call-update) | async-done | bytes 524304 | tf_op jit(solution)/shard_map/psum | solution.py:54
  184.5 1.9 copy.27
  (14 shorter events, 1.0 us)
Async XLA Ops:
  6.5 65.4 %reduce-scatter.2.cloned.1.call-start = ((), (), s32[]{:S(2)}) async-start(), calls=%async_computation.1 | async-start | bytes 589824 | tf_op jit(solution)/shard_map/reduce_scatter | solution.py:37
  37.7 59.9 %all-gather.3.cloned.1.call-start = ((), (), s32[]{:S(2)}) async-start(), calls=%async_computation.2 | async-start | bytes 1179648 | tf_op jit(solution)/shard_map/all_gather | solution.py:49
  38.4 87.2 %all-gather.5.cloned.1.call-start = ((), (), s32[]{:S(2)}) async-start(), calls=%async_computation.3 | async-start | bytes 2359296 | tf_op jit(solution)/shard_map/all_gather | solution.py:50
  39.2 145.4 %all-reduce.2.cloned.1.call-start = ((), (), s32[]{:S(2)}) async-start(), calls=%async_computation.4 | async-start | bytes 1048576 | tf_op jit(solution)/shard_map/psum | solution.py:54
  138.8 0.8 copy-start
Sparse Core Ops, SparseCore 0:
  37.8 34.0 reduce-scatter.1
  73.5 21.7 all-gather.2
  96.9 28.6 all-gather.4
  139.7 44.7 all-reduce.1
where the time goes:
time: 193 us
  waiting for transfers between devices  105 us (54%)
  matrix products  49 us (25%)
  blocking collectives  16.8 us (9%)
  between operations  13.2 us (7%)
  local copies, waits for them, and re-layouts  4.92 us (3%)
  other arithmetic  4.13 us (2%)
    psum x1, waiting for transfers between devices, on_device(): return lax.psum(back + placed, 'dp')  44.9 us
    reduce_scatter x1, waiting for transfers between devices, on_device(): lax.psum_scatter(forward_part.astype(jnp.bfloat16), 'centers', scatter_di...  31.9 us
    all_gather x1, waiting for transfers between devices, on_device(): piece_coef = lax.all_gather(coef, 'centers', axis=0, tiled=True)  26.4 us
    dot_general x4, matrix products, kernel_block(): lax.dot_general(left_pts, right_pts, (((1,), (1,)), ((), ())), preferred_...  17.6 us
    all_gather x1, blocking collectives, on_device(): forward = lax.all_gather(shared, 'centers', axis=0, tiled=True)  16.8 us
    dot_general x1, matrix products, on_device(): regular = jnp.dot(kernel, piece_coef, preferred_element_type=jnp.float32)  13.2 us
    dot_general x4, matrix products, forward_keep(): jnp.dot(kernel, coef, preferred_element_type=jnp.float32)  9.35 us
    dot_general x1, matrix products, on_device(): jnp.einsum('bij,bio->jo', tiles, forward_blocks, preferred_element_type=j...  8.89 us
  transfers between devices with their start and end apart: 4, of which 3 were waited for; matrix products, arithmetic and copies ran while one was open for 6% of the time, Pallas kernels for 0%

commit v1 on v0

--- a/solution.py
+++ b/solution.py
@@ -51,7 +51,7 @@
     kernel = kernel_block(own_cen, own_sq, piece_cen, squares(piece_cen), features)
     regular = jnp.dot(kernel, piece_coef, preferred_element_type=jnp.float32)
     placed = lax.dynamic_update_slice_in_dim(jnp.zeros_like(back), regular, own_start, 0)
-    return lax.psum(back + placed, "dp")
+    return jnp.sum(lax.all_gather(back + placed, "dp"), axis=0)
 
 
 def solution(mesh):

time: 193 us -> 184 us (0.953)
  waiting for transfers between devices: 105 us -> 94.4 us
  other arithmetic: 4.13 us -> 6.68 us
    psum x1 -> x0, waiting for transfers between devices: 44.9 us -> none  [on_device(): return lax.psum(back + placed, 'dp')]
    all_gather x0 -> x1, waiting for transfers between devices: none -> 34.7 us  [on_device(): return jnp.sum(lax.all_gather(back + placed, 'dp'), axis=0)]
    reduce_sum x0 -> x1, other arithmetic: none -> 2.55 us  [on_device(): return jnp.sum(lax.all_gather(back + placed, 'dp'), axis=0)]
where the time goes in v1:
time: 184 us; the launch traced here: 183 us
  waiting for transfers between devices  94.4 us (51%)
  matrix products  49 us (27%)
  blocking collectives  16.8 us (9%)
  between operations  13.2 us (7%)
  other arithmetic  6.68 us (4%)
  local copies, waits for them, and re-layouts  3.09 us (2%)
    all_gather x1, waiting for transfers between devices, on_device(): return jnp.sum(lax.all_gather(back + placed, 'dp'), axis=0)  34.7 us
    reduce_scatter x1, waiting for transfers between devices, on_device(): lax.psum_scatter(forward_part.astype(jnp.bfloat16), 'centers', scatter_di...  31.9 us
    all_gather x1, waiting for transfers between devices, on_device(): piece_coef = lax.all_gather(coef, 'centers', axis=0, tiled=True)  26.4 us
    dot_general x4, matrix products, kernel_block(): lax.dot_general(left_pts, right_pts, (((1,), (1,)), ((), ())), preferred_...  17.6 us
    all_gather x1, blocking collectives, on_device(): forward = lax.all_gather(shared, 'centers', axis=0, tiled=True)  16.8 us
    dot_general x1, matrix products, on_device(): regular = jnp.dot(kernel, piece_coef, preferred_element_type=jnp.float32)  13.2 us
    dot_general x4, matrix products, forward_keep(): jnp.dot(kernel, coef, preferred_element_type=jnp.float32)  9.35 us
    dot_general x1, matrix products, on_device(): jnp.einsum('bij,bio->jo', tiles, forward_blocks, preferred_element_type=j...  8.89 us
  transfers between devices with their start and end apart: 4, of which 3 were waited for; matrix products, arithmetic and copies ran while one was open for 6% of the time, Pallas kernels for 0%

profile of v1, /device:TPU:0, one launch (start us, length us, event | category | flops | bytes accessed | tf_op | source)
XLA Modules:
  0.0 183.4 jit_solution(5461382110267612983)
XLA Ops:
  6.5 1.4 copy.8
  8.0 1.0 multiply_reduce_fusion.2
  8.9 27.9 %while.12 = (s32[]{:T(128)}, bf16[4,1024,2048]{2,1,0:T(8,128)(2,1)}, bf16[4,1024,64]{1,2,0:T(8,128)(2,1)S(1)}, bf16[4,1024,32]{2,1,0:T(8,128)(2,1)S(1)}, f32[204...) while((s32[]{:T(128)}, bf16[4,1024,2048]{2,1,0:T(8,128)(2,1)}, ...), condition=%wide.region_3.4_spmd, body=%wide.region_1.3_spmd.sunk | while | flops 413236224 | bytes 13583461 | solution.py:35
  9.2 4.4 %bitcast_dynamic-update-slice_fusion.2 = (bf16[4,1024,2048]{2,1,0:T(8,128)(2,1)}, bf16[1024,2048]{1,0:T(8,128)(2,1)S(1)}) fusion(bf16[4,1024,2048]{2,1,0:T(8,128)(2,1)} %get-tuple-element.117, s32[]{:T(128)S(6)} %copy.22, bf16[2048,32]{0,1:T(8,128)(2,1)} %get-tuple-element.129, bf16[4,1024,32]{2,1,0:T(8,128)(2,1)S(1)} %get-tuple-element.127, ...), kind=kOutput, calls=%fused_computation.1.clone.1 | convolution fusion | flops 144703488 | bytes 8795136 | tf_op jit(solution)/shard_map/while/body/eval_jaxpr/dot_general | solution.py:8
  13.5 2.3 %fusion.30 = bf16[4,1024,64]{1,2,0:T(8,128)(2,1)S(1)} fusion(bf16[4,1024,64]{1,2,0:T(8,128)(2,1)S(1)} %get-tuple-element.118, s32[]{:T(128)S(6)} %copy.22, bf16[1024,2048]{1,0:T(8,128)(2,1)S(1)} %get-tuple-element.107, bf16[2048,64]{0,1:T(8,128)(2,1)} %get-tuple-element.130), kind=kOutput, calls=%fused_computation.3.clone.1 | convolution fusion | flops 268435456 | bytes 4718596 | tf_op jit(solution)/shard_map/while/body/eval_jaxpr/dot_general | solution.py:33
  16.1 4.4 %bitcast_dynamic-update-slice_fusion.2 = (bf16[4,1024,2048]{2,1,0:T(8,128)(2,1)}, bf16[1024,2048]{1,0:T(8,128)(2,1)S(1)}) fusion(bf16[4,1024,2048]{2,1,0:T(8,128)(2,1)} %get-tuple-element.117, s32[]{:T(128)S(6)} %copy.22, bf16[2048,32]{0,1:T(8,128)(2,1)} %get-tuple-element.129, bf16[4,1024,32]{2,1,0:T(8,128)(2,1)S(1)} %get-tuple-element.127, ...), kind=kOutput, calls=%fused_computation.1.clone.1 | convolution fusion | flops 144703488 | bytes 8795136 | tf_op jit(solution)/shard_map/while/body/eval_jaxpr/dot_general | solution.py:8
  20.5 2.3 %fusion.30 = bf16[4,1024,64]{1,2,0:T(8,128)(2,1)S(1)} fusion(bf16[4,1024,64]{1,2,0:T(8,128)(2,1)S(1)} %get-tuple-element.118, s32[]{:T(128)S(6)} %copy.22, bf16[1024,2048]{1,0:T(8,128)(2,1)S(1)} %get-tuple-element.107, bf16[2048,64]{0,1:T(8,128)(2,1)} %get-tuple-element.130), kind=kOutput, calls=%fused_computation.3.clone.1 | convolution fusion | flops 268435456 | bytes 4718596 | tf_op jit(solution)/shard_map/while/body/eval_jaxpr/dot_general | solution.py:33
  23.1 4.4 %bitcast_dynamic-update-slice_fusion.2 = (bf16[4,1024,2048]{2,1,0:T(8,128)(2,1)}, bf16[1024,2048]{1,0:T(8,128)(2,1)S(1)}) fusion(bf16[4,1024,2048]{2,1,0:T(8,128)(2,1)} %get-tuple-element.117, s32[]{:T(128)S(6)} %copy.22, bf16[2048,32]{0,1:T(8,128)(2,1)} %get-tuple-element.129, bf16[4,1024,32]{2,1,0:T(8,128)(2,1)S(1)} %get-tuple-element.127, ...), kind=kOutput, calls=%fused_computation.1.clone.1 | convolution fusion | flops 144703488 | bytes 8795136 | tf_op jit(solution)/shard_map/while/body/eval_jaxpr/dot_general | solution.py:8
  27.5 2.3 %fusion.30 = bf16[4,1024,64]{1,2,0:T(8,128)(2,1)S(1)} fusion(bf16[4,1024,64]{1,2,0:T(8,128)(2,1)S(1)} %get-tuple-element.118, s32[]{:T(128)S(6)} %copy.22, bf16[1024,2048]{1,0:T(8,128)(2,1)S(1)} %get-tuple-element.107, bf16[2048,64]{0,1:T(8,128)(2,1)} %get-tuple-element.130), kind=kOutput, calls=%fused_computation.3.clone.1 | convolution fusion | flops 268435456 | bytes 4718596 | tf_op jit(solution)/shard_map/while/body/eval_jaxpr/dot_general | solution.py:33
  30.1 4.4 %bitcast_dynamic-update-slice_fusion.2 = (bf16[4,1024,2048]{2,1,0:T(8,128)(2,1)}, bf16[1024,2048]{1,0:T(8,128)(2,1)S(1)}) fusion(bf16[4,1024,2048]{2,1,0:T(8,128)(2,1)} %get-tuple-element.117, s32[]{:T(128)S(6)} %copy.22, bf16[2048,32]{0,1:T(8,128)(2,1)} %get-tuple-element.129, bf16[4,1024,32]{2,1,0:T(8,128)(2,1)S(1)} %get-tuple-element.127, ...), kind=kOutput, calls=%fused_computation.1.clone.1 | convolution fusion | flops 144703488 | bytes 8795136 | tf_op jit(solution)/shard_map/while/body/eval_jaxpr/dot_general | solution.py:8
  34.5 2.3 %fusion.30 = bf16[4,1024,64]{1,2,0:T(8,128)(2,1)S(1)} fusion(bf16[4,1024,64]{1,2,0:T(8,128)(2,1)S(1)} %get-tuple-element.118, s32[]{:T(128)S(6)} %copy.22, bf16[1024,2048]{1,0:T(8,128)(2,1)S(1)} %get-tuple-element.107, bf16[2048,64]{0,1:T(8,128)(2,1)} %get-tuple-element.130), kind=kOutput, calls=%fused_computation.3.clone.1 | convolution fusion | flops 268435456 | bytes 4718596 | tf_op jit(solution)/shard_map/while/body/eval_jaxpr/dot_general | solution.py:33
  36.8 0.8 copy.12
  37.7 0.7 all-gather.4.cloned.1.call-update
  38.5 0.7 all-gather.6.cloned.1.call-update
  39.2 0.8 multiply_reduce_fusion.3
  40.0 31.9 %reduce-scatter.2.cloned.1.call-done = bf16[512,64]{0,1:T(8,128)(2,1)} async-done(((bf16[4096,64]{0,1:T(8,128)(2,1)}), bf16[512,64]{0,1:T(8,128)(2,1)}) %reduce-scatter.2.cloned.1.call-update) | async-done | bytes 65552 | tf_op jit(solution)/shard_map/reduce_scatter | solution.py:37
  71.9 16.8 %all_gather.17 = bf16[4096,64]{0,1:T(8,128)(2,1)S(1)} all-gather(bf16[512,64]{0,1:T(8,128)(2,1)} %reduce-scatter.2.cloned.1.call-done), channel_id=1, replica_groups=mesh['dp'=4,'centers'=8] {'centers'}, dimensions={0}, use_global_device_ids=true | all-gather | bytes 589824 | tf_op jit(solution)/shard_map/all_gather | solution.py:40
  88.7 8.9 %fusion.5 = f32[2048,64]{0,1:T(8,128)S(1)} fusion(bf16[4,1024,2048]{2,1,0:T(8,128)(2,1)} %get-tuple-element.43, bf16[8,4,8,1024]{3,2,1,0:T(8,128)(2,1)S(1)} %bitcast.52), kind=kOutput, calls=%fused_computation.11 | convolution fusion | flops 1073872896 | bytes 17825792 | tf_op jit(solution)/shard_map/bij,bio->jo/dot_general | solution.py:42
  97.7 1.5 multiply_reduce_fusion.1
  99.2 26.4 %all-gather.6.cloned.1.call-done = bf16[16384,64]{0,1:T(8,128)(2,1)} async-done(((bf16[2048,64]{0,1:T(8,128)(2,1)}), bf16[16384,64]{0,1:T(8,128)(2,1)}) %all-gather.6.cloned.1.call-update) | async-done | bytes 2097168 | tf_op jit(solution)/shard_map/all_gather | solution.py:50
  125.6 13.2 %fusion.8 = f32[1,2048,64]{1,2,0:T(8,128)S(1)} fusion(f32[1,2048,64]{1,2,0:T(8,128)S(1)} %copy.28, s32[]{:T(128)S(6)} %select_n.4, bf16[16384,64]{0,1:T(8,128)(2,1)} %all-gather.6.cloned.1.call-done, bf16[16384,32]{0,1:T(8,128)(2,1)} %all-gather.4.cloned.1.call-done, f32[16384]{0:T(1024)S(1)} %multiply_reduce_fusion.1, f32[512]{0:T(512)S(1)} %multiply_reduce_fusion.3, ...), kind=kOutput, calls=%fused_computation.15 | convolution fusion | flops 1652588544 | bytes 3509248 | tf_op jit(solution)/shard_map/dot_general | solution.py:52
  138.8 0.8 copy-done
  139.6 34.7 %all-gather.8.cloned.1.call-done = f32[4,2048,64]{1,2,0:T(8,128)} async-done(((f32[1,2048,64]{1,2,0:T(8,128)}), f32[4,2048,64]{1,2,0:T(8,128)}) %all-gather.8.cloned.1.call-update) | async-done | bytes 2097168 | tf_op jit(solution)/shard_map/all_gather | solution.py:54
  174.3 2.6 %reduce_sum.48 = f32[2048,64]{0,1:T(8,128)} reduce(f32[4,2048,64]{1,2,0:T(8,128)} %all-gather.8.cloned.1.call-done, f32[]{:T(128)} %constant.13.clone.1), dimensions={0}, to_apply=%region_7.8 | reduce | flops 393216 | bytes 2621444 | tf_op jit(solution)/shard_map/reduce_sum | solution.py:54
  (15 shorter events, 1.1 us)
Async XLA Ops:
  6.5 65.4 %reduce-scatter.2.cloned.1.call-start = ((), (), s32[]{:S(2)}) async-start(), calls=%async_computation.1 | async-start | bytes 589824 | tf_op jit(solution)/shard_map/reduce_scatter | solution.py:37
  37.7 60.0 %all-gather.4.cloned.1.call-start = ((), (), s32[]{:S(2)}) async-start(), calls=%async_computation.2 | async-start | bytes 1179648 | tf_op jit(solution)/shard_map/all_gather | solution.py:49
  38.4 87.2 %all-gather.6.cloned.1.call-start = ((), (), s32[]{:S(2)}) async-start(), calls=%async_computation.3 | async-start | bytes 2359296 | tf_op jit(solution)/shard_map/all_gather | solution.py:50
  39.2 135.2 %all-gather.8.cloned.1.call-start = ((), (), s32[]{:S(2)}) async-start(), calls=%async_computation.4 | async-start | bytes 2621440 | tf_op jit(solution)/shard_map/all_gather | solution.py:54
  138.8 0.8 copy-start
Sparse Core Ops, SparseCore 0:
  37.8 34.0 reduce-scatter.1
  73.5 21.7 all-gather.3
  96.9 28.6 all-gather.5
  139.7 34.5 all-gather.7
